TPU v7x, 128 devices: a whole 4x4x4 slice. The times are simulated.
128 devices in a mesh: expert: 128 (over y, x, z, core).
Axes of the slice: x: 4, y: 4, z: 4, core: 2. Of those that a mesh axis runs over, the one named last changes fastest.
Arguments:
- tokens: bfloat16 [16384, 4096], P('expert'), may hold values from -6 to 6
- norm_gain: float32 [4096], replicated, may hold values from 0.5 to 1.5
- router_weight: bfloat16 [4096, 128], replicated, may hold values from -0.09375 to 0.09375
- expert_ids: int32 [16384, 2], P('expert'), may hold values from 0 to 127, as said below
- gate_proj: bfloat16 [128, 4096, 768], P('expert'), may hold values from -0.09375 to 0.09375
- up_proj: bfloat16 [128, 4096, 768], P('expert'), may hold values from -0.09375 to 0.09375
- down_proj: bfloat16 [128, 768, 4096], P('expert'), may hold values from -0.21875 to 0.21875
- value_weight: bfloat16 [4096], replicated, may hold values from -0.09375 to 0.09375
- value_target: int32 [16384], P('expert'), may hold values from -1 to 1
- recency: float32 [16384], P('expert'), may hold values from 0.25 to 18, as said below
Outputs:
- mixed: bfloat16 [16384, 4096], P('expert')
- values: float32 [16384], P('expert')
- loss: float32 [], replicated
Inputs may be any that keep to these rules, and one draw needn't show every extreme that they name: `expert_ids`: each row names two different experts; among the rows of one device no expert is named more than 3 times. `recency`: positive weights.
All inputs are finite; a program needn't handle non-finite values.
Results may differ from a plain program's by a relative error of at most 0.0055.
Values may be sent and summed in bfloat16 or wider, within the bound.
No kernel may reach another device: no remote copies, remote signals or barrier semaphores. Data moves between devices by JAX's collectives and lax.ppermute only.
A program may use at most 128 MiB of HBM per device.

v0:
```python
import jax
import jax.numpy as jnp
from jax import lax
from jax.sharding import Mesh
from jax.sharding import PartitionSpec as P

EXPERT = ("expert_0", "expert_1", "expert_2", "expert_3")


def by_axis(x, axes):
    for axis in axes:
        x = lax.psum(x, axis)
    return x


def expert_ffn(received, gate_proj, up_proj, down_proj):
    sources, slots, width = received.shape
    flat_input = received.reshape(sources * slots, width)
    gate_part = jnp.dot(flat_input, gate_proj[0], preferred_element_type=jnp.float32)
    up_part = jnp.dot(flat_input, up_proj[0], preferred_element_type=jnp.float32)
    hidden = (jax.nn.silu(gate_part) * up_part).astype(jnp.bfloat16)
    result = jnp.dot(hidden, down_proj[0], preferred_element_type=jnp.float32).astype(jnp.bfloat16)
    return result.reshape(sources, slots, width)


def body(
    tokens,
    norm_gain,
    router_weight,
    expert_ids,
    gate_proj,
    up_proj,
    down_proj,
    value_weight,
    value_target,
    recency,
):
    token_count, width = tokens.shape
    expert_total = router_weight.shape[1]
    capacity = 3 * token_count // expert_total
    wide = tokens.astype(jnp.float32)
    inverse = lax.rsqrt(jnp.mean(wide * wide, axis=1, keepdims=True) + 1e-05)
    normed = (wide * inverse * norm_gain).astype(jnp.bfloat16)
    logits = jnp.dot(normed, router_weight, preferred_element_type=jnp.float32)
    columns = lax.broadcasted_iota(jnp.int32, (1, expert_total), 1)
    first = jnp.sum(jnp.where(expert_ids[:, 0:1] == columns, logits, 0.0), axis=1)
    second = jnp.sum(jnp.where(expert_ids[:, 1:2] == columns, logits, 0.0), axis=1)
    gate_first = jax.nn.sigmoid(first - second)
    gate_second = jax.nn.sigmoid(second - first)
    flat_ids = expert_ids.reshape(-1)
    one_hot = (flat_ids[:, None] == columns).astype(jnp.int32)
    slot_rank = jnp.sum(jnp.cumsum(one_hot, axis=0) * one_hot, axis=1) - 1
    slot_index = flat_ids * capacity + slot_rank
    row_index = jnp.arange(2 * token_count, dtype=jnp.int32) // 2
    source_row = (
        jnp.full((expert_total * capacity,), token_count, dtype=jnp.int32)
        .at[slot_index]
        .set(row_index)
    )
    padded = jnp.concatenate([normed, jnp.zeros((1, width), jnp.bfloat16)], axis=0)
    outgoing = padded[source_row].reshape(expert_total, capacity, width)
    received = lax.all_to_all(outgoing, EXPERT, split_axis=0, concat_axis=0, tiled=True)
    produced = expert_ffn(received, gate_proj, up_proj, down_proj)
    returned = lax.all_to_all(produced, EXPERT, split_axis=0, concat_axis=0, tiled=True)
    flat_back = returned.reshape(expert_total * capacity, width)
    picked = flat_back[slot_index].reshape(token_count, 2, width)
    mixed = (
        wide
        + gate_first[:, None] * picked[:, 0].astype(jnp.float32)
        + gate_second[:, None] * picked[:, 1].astype(jnp.float32)
    ).astype(jnp.bfloat16)
    values = jnp.tanh(jnp.dot(mixed, value_weight, preferred_element_type=jnp.float32))
    error = values - value_target.astype(jnp.float32)
    weighted, weight_total = (
        by_axis(jnp.sum(recency * error * error), EXPERT),
        by_axis(jnp.sum(recency), EXPERT),
    )
    loss = weighted / weight_total
    return (mixed, values, loss)


def solution(mesh):
    finer = Mesh(mesh.devices.reshape(4, 4, 4, 2), ("expert_0", "expert_1", "expert_2", "expert_3"))
    in_specs = (
        P(EXPERT, None),
        P(),
        P(),
        P(EXPERT, None),
        P(EXPERT, None, None),
        P(EXPERT, None, None),
        P(EXPERT, None, None),
        P(),
        P(EXPERT),
        P(EXPERT),
    )
    out_specs = (P(EXPERT, None), P(EXPERT), P())
    return jax.shard_map(body, mesh=finer, in_specs=in_specs, out_specs=out_specs, check_vma=False)
```

profile of v0, /device:TPU:1, one launch (start us, length us, event | category | flops | bytes accessed | tf_op | source)
XLA Modules:
  0.0 242.7 jit_solution(9639308537524238652)
XLA Ops:
  0.6 0.0 copy-start
  0.6 0.0 copy-start.1
  0.7 0.0 copy-start.4
  0.7 0.8 broadcast_multiply_fusion
  1.5 0.8 copy.14
  2.3 0.1 eq.67
  2.4 0.1 eq.63
  2.6 1.5 fusion.9
  4.1 0.1 copy.13
  4.2 0.1 mul.75
  4.4 0.1 copy.16
  4.5 0.2 fusion.24
  4.8 0.2 fusion.25
  5.0 1.4 scatter_custom_fusion
  6.4 0.0 copy-done.1
  6.4 0.0 copy-done.4
  6.4 0.3 fusion.11
  6.8 0.1 concatenate.3
  6.9 4.1 %gather_fusion = bf16[384,4096]{1,0:T(8,128)(2,1)} fusion(bf16[129,4096]{1,0:T(8,128)(2,1)S(1)} %concatenate.3, s32[1024]{0:T(1024)S(1)} %pad_clamp_fusion.1), kind=kCustom, calls=%fused_computation | custom fusion | bytes 6292992 | tf_op jit(solution)/shard_map/gather | solution.py:61
  10.9 7.1 %reshape.104 = bf16[128,3,4096]{2,1,0:T(4,128)(2,1)} reshape(bf16[384,4096]{1,0:T(8,128)(2,1)} %gather_fusion) | data formatting | bytes 6291456 | tf_op jit(solution)/shard_map/reshape | solution.py:61
  18.0 64.2 %all_to_all.10 = bf16[128,3,4096]{2,1,0:T(4,128)(2,1)} all-to-all(bf16[128,3,4096]{2,1,0:T(4,128)(2,1)} %reshape.104), channel_id=1, replica_groups=mesh['expert_0'=4,'expert_1'=4,'expert_2'=4,'expert_3'=2] {'expert_0','e..., dimensions={0} | all-to-all | bytes 6291456 | tf_op jit(solution)/shard_map/all_to_all | solution.py:62
  82.2 7.4 %reshape.105 = bf16[384,4096]{1,0:T(8,128)(2,1)} reshape(bf16[128,3,4096]{2,1,0:T(4,128)(2,1)} %all_to_all.10) | data formatting | bytes 6291456 | tf_op jit(solution)/shard_map/reshape | solution.py:18
  89.6 7.4 %fusion.4 = f32[384,768]{1,0:T(8,128)} fusion(bf16[384,4096]{1,0:T(8,128)(2,1)} %reshape.105, bf16[1,4096,768]{2,1,0:T(8,128)(2,1)} %param.14), kind=kOutput, calls=%fused_computation.7 | convolution fusion | flops 2415919104 | bytes 10616832 | tf_op jit(solution)/shard_map/dot_general | solution.py:19
  97.0 14.2 %fusion.6 = bf16[384,4096]{1,0:T(8,128)(2,1)} fusion(bf16[1,768,4096]{2,1,0:T(8,128)(2,1)} %param.16, bf16[384,4096]{1,0:T(8,128)(2,1)} %reshape.105, bf16[1,4096,768]{2,1,0:T(8,128)(2,1)} %param.15, f32[384,768]{1,0:T(8,128)} %fusion.4), kind=kOutput, calls=%fused_computation.9 | convolution fusion | flops 4835180544 | bytes 20054016 | tf_op jit(solution)/shard_map/dot_general | solution.py:22
  111.2 7.1 %reshape.106 = bf16[128,3,4096]{2,1,0:T(4,128)(2,1)} reshape(bf16[384,4096]{1,0:T(8,128)(2,1)} %fusion.6) | data formatting | bytes 6291456 | tf_op jit(solution)/shard_map/reshape | solution.py:23
  118.3 0.0 copy-start.6
  118.3 0.0 copy-start.5
  118.3 6.1 %all-to-all-start.1 = ((bf16[128,3,4096]{2,1,0:T(4,128)(2,1)}), bf16[128,3,4096]{2,1,0:T(4,128)(2,1)}, u32[]{:S(2)}, u32[]{:S(2)}) async-start(bf16[128,3,4096]{2,1,0:T(4,128)(2,1)} %reshape.106), calls=%async_computation.1 | async-start | bytes 8388608 | tf_op jit(solution)/shard_map/all_to_all | solution.py:64
  124.4 0.0 copy-done.6
  124.4 0.0 copy-done.5
  124.5 0.0 copy-done
  124.5 0.5 select_reduce_fusion.1
  125.0 51.7 %all-to-all-done.1 = bf16[128,3,4096]{2,1,0:T(4,128)(2,1)} async-done(((bf16[128,3,4096]{2,1,0:T(4,128)(2,1)}), bf16[128,3,4096]{2,1,0:T(4,128)(2,1)}, u32[]{:S(2)}, u32[]{:S(2)}) %all-to-all-start.1) | async-done | bytes 3145760 | tf_op jit(solution)/shard_map/all_to_all | solution.py:64
  176.8 7.4 %reshape.107 = bf16[384,4096]{1,0:T(8,128)(2,1)} reshape(bf16[128,3,4096]{2,1,0:T(4,128)(2,1)} %all-to-all-done.1) | data formatting | bytes 6291456 | tf_op jit(solution)/shard_map/reshape | solution.py:65
  184.2 7.5 %gather_fusion.1 = bf16[256,4096]{1,0:T(8,128)(2,1)} fusion(bf16[384,4096]{1,0:T(8,128)(2,1)} %reshape.107, s32[1024]{0:T(1024)S(1)} %pad_clamp_fusion), kind=kCustom, calls=%fused_computation.1 | custom fusion | bytes 4195328 | tf_op jit(solution)/shard_map/gather | solution.py:66
  191.7 3.2 %reshape.108 = bf16[128,2,4096]{2,1,0:T(2,128)(2,1)S(1)} reshape(bf16[256,4096]{1,0:T(8,128)(2,1)} %gather_fusion.1) | data formatting | bytes 4194304 | tf_op jit(solution)/shard_map/reshape | solution.py:66
  194.9 0.0 copy-start.2
  194.9 4.7 %fusion.33 = (bf16[128,1,4096]{2,1,0:T(2,128)(2,1)S(1)}, bf16[128,1,4096]{2,1,0:T(2,128)(2,1)S(1)}) fusion(bf16[128,2,4096]{2,1,0:T(2,128)(2,1)S(1)} %reshape.108), kind=kLoop, calls=%fused_computation.61 | loop fusion | bytes 4194304 | tf_op jit(solution)/shard_map/slice | solution.py:69
  199.6 0.0 copy-done.2
  199.6 0.0 copy-start.7
  199.6 0.0 copy-start.8
  199.6 4.2 %fusion.13 = bf16[128,4096]{1,0:T(8,128)(2,1)S(1)} fusion(bf16[128,4096]{1,0:T(8,128)(2,1)S(1)} %copy-done.2, bf16[128,1,4096]{2,1,0:T(2,128)(2,1)S(1)} %get-tuple-element.16, bf16[128,1,4096]{2,1,0:T(2,128)(2,1)S(1)} %get-tuple-element.15, f32[128]{0:T(128)S(1)} %get-tuple-element.18, f32[128]{0:T(128)S(1)} %get-tuple-element.17), kind=kLoop, calls=%fused_computation.17 | loop fusion | flops 4194304 | bytes 4195328 | tf_op jit(solution)/shard_map/convert_element_type | solution.py:71
  203.8 0.0 copy-done.7
  203.8 0.0 copy-done.8
  203.8 0.0 copy-start.3
  203.8 1.5 fusion.32
  205.3 7.5 %all-reduce.3 = (f32[]{:T(128)}, f32[]{:T(128)}) all-reduce(f32[]{:T(128)} %get-tuple-element.6, f32[]{:T(128)} %get-tuple-element.5), channel_id=1, replica_groups=mesh['expert_0'=4,'expert_1'=4,'expert_2'=4,'expert_3'=2] {'expert_0'}, use_global_device_ids=true, to_apply=%region_8.9 | all-reduce | flops 2 | bytes 16 | tf_op jit(solution)/shard_map/psum | solution.py:12
  212.8 7.5 %all-reduce.2 = (f32[]{:T(128)}, f32[]{:T(128)}) all-reduce(f32[]{:T(128)} %get-tuple-element.11, f32[]{:T(128)} %get-tuple-element.12), channel_id=1, replica_groups=mesh['expert_0'=4,'expert_1'=4,'expert_2'=4,'expert_3'=2] {'expert_1'}, use_global_device_ids=true, to_apply=%region_9.10 | all-reduce | flops 2 | bytes 16 | tf_op jit(solution)/shard_map/psum | solution.py:12
  220.3 8.0 %all-reduce.1 = (f32[]{:T(128)}, f32[]{:T(128)}) all-reduce(f32[]{:T(128)} %get-tuple-element.9, f32[]{:T(128)} %get-tuple-element.10), channel_id=1, replica_groups=mesh['expert_0'=4,'expert_1'=4,'expert_2'=4,'expert_3'=2] {'expert_2'}, use_global_device_ids=true, to_apply=%region_10.11 | all-reduce | flops 2 | bytes 16 | tf_op jit(solution)/shard_map/psum | solution.py:12
  228.3 12.0 %all-reduce.4 = (f32[]{:T(128)}, f32[]{:T(128)}) all-reduce(f32[]{:T(128)} %get-tuple-element.7, f32[]{:T(128)} %get-tuple-element.8), channel_id=1, replica_groups=mesh['expert_0'=4,'expert_1'=4,'expert_2'=4,'expert_3'=2] {'expert_3'}, use_global_device_ids=true, to_apply=%region_11.12 | all-reduce | flops 2 | bytes 16 | tf_op jit(solution)/shard_map/psum | solution.py:12
  241.5 0.0 copy-done.3
  (16 shorter events, 0.1 us)
Async XLA Ops:
  0.6 123.8 %copy-start = (bf16[4096,128]{1,0:T(8,128)(2,1)S(1)}, bf16[4096,128]{1,0:T(8,128)(2,1)}, u32[]{:S(2)}) copy-start(bf16[4096,128]{1,0:T(8,128)(2,1)} %param.12) | copy-start | bytes 3145732
  0.6 5.8 %copy-start.1 = (bf16[128,4096]{1,0:T(8,128)(2,1)S(1)}, bf16[128,4096]{1,0:T(8,128)(2,1)}, u32[]{:S(2)}) copy-start(bf16[128,4096]{1,0:T(8,128)(2,1)} %param.10) | copy-start | bytes 3145732
  0.7 5.8 %copy-start.4 = (f32[4096]{0:T(1024)S(1)}, f32[4096]{0:T(1024)}, u32[]{:S(2)}) copy-start(f32[4096]{0:T(1024)} %param.11) | copy-start | bytes 49156
  118.3 6.1 %copy-start.6 = (bf16[4096]{0:T(1024)(128)(2,1)S(1)}, bf16[4096]{0:T(1024)(128)(2,1)}, u32[]{:S(2)}) copy-start(bf16[4096]{0:T(1024)(128)(2,1)} %param.17) | copy-start | bytes 24580
  118.3 6.2 %copy-start.5 = (s32[128,2]{0,1:T(2,128)S(1)}, s32[128,2]{0,1:T(2,128)}, u32[]{:S(2)}) copy-start(s32[128,2]{0,1:T(2,128)} %param.13) | copy-start | bytes 3076
  118.3 58.5 %all-to-all-start.1 = ((bf16[128,3,4096]{2,1,0:T(4,128)(2,1)}), bf16[128,3,4096]{2,1,0:T(4,128)(2,1)}, u32[]{:S(2)}, u32[]{:S(2)}) async-start(bf16[128,3,4096]{2,1,0:T(4,128)(2,1)} %reshape.106), calls=%async_computation.1 | async-start | bytes 8388608 | tf_op jit(solution)/shard_map/all_to_all | solution.py:64
  194.9 4.7 %copy-start.2 = (bf16[128,4096]{1,0:T(8,128)(2,1)S(1)}, bf16[128,4096]{1,0:T(8,128)(2,1)}, u32[]{:S(2)}) copy-start(bf16[128,4096]{1,0:T(8,128)(2,1)} %param.10) | copy-start | bytes 3145732
  199.6 4.2 %copy-start.7 = (f32[128]{0:T(128)S(1)}, f32[128]{0:T(128)}, u32[]{:S(2)}) copy-start(f32[128]{0:T(128)} %param.19) | copy-start | bytes 1540
  199.6 4.2 %copy-start.8 = (s32[128]{0:T(128)S(1)}, s32[128]{0:T(128)}, u32[]{:S(2)}) copy-start(s32[128]{0:T(128)} %param.18) | copy-start | bytes 1540
  203.8 37.7 %copy-start.3 = (bf16[128,4096]{1,0:T(8,128)(2,1)}, bf16[128,4096]{1,0:T(8,128)(2,1)S(1)}, u32[]{:S(2)}) copy-start(bf16[128,4096]{1,0:T(8,128)(2,1)S(1)} %fusion.13) | copy-start | bytes 3145732
where the time goes:
time: 244 us; the launch traced here: 243 us
  blocking collectives  99.1 us (41%)
  waiting for transfers between devices  51.7 us (21%)
  local copies, waits for them, and re-layouts  51.4 us (21%)
  matrix products  23.6 us (10%)
  other arithmetic  7.35 us (3%)
  starting transfers between devices  6.1 us (2%)
  between operations  3.29 us (1%)
    all_to_all x1, blocking collectives, body(): lax.all_to_all(outgoing, EXPERT, split_axis=0, concat_axis=0, tiled=True)  64.2 us
    all_to_all x1, waiting for transfers between devices, body(): lax.all_to_all(produced, EXPERT, split_axis=0, concat_axis=0, tiled=True)  51.7 us
    psum x4, blocking collectives, by_axis(): x = lax.psum(x, axis)  34.9 us
    dot_general x1, matrix products, expert_ffn(): jnp.dot(hidden, down_proj[0], preferred_element_type=jnp.float32)  14.2 us
    gather x1, local copies, waits for them, and re-layouts, body(): picked = flat_back[slot_index].reshape(token_count, 2, width)  7.53 us
    reshape x1, local copies, waits for them, and re-layouts, body(): flat_back = returned.reshape(expert_total * capacity, width)  7.42 us
    reshape x1, local copies, waits for them, and re-layouts, expert_ffn(): flat_input = received.reshape(sources * slots, width)  7.4 us
    dot_general x1, matrix products, expert_ffn(): jnp.dot(flat_input, gate_proj[0], preferred_element_type=jnp.float32)  7.38 us
  transfers between devices with their start and end apart: 1, of which 1 were waited for; matrix products, arithmetic and copies ran while one was open for 0% of the time, Pallas kernels for 0%

commit v1 on v0

--- a/solution.py
+++ b/solution.py
@@ -9,7 +9,8 @@
 
 def by_axis(x, axes):
     for axis in axes:
-        x = lax.psum(x, axis)
+        terms = lax.all_gather(x, axis, axis=0, tiled=False)
+        x = terms.sum(axis=0)
     return x
 
 

time: 244 us -> 260 us (1.066)
  local copies, waits for them, and re-layouts: 51.4 us -> 65.1 us
  other arithmetic: 7.35 us -> 12.2 us
  blocking collectives: 99.1 us -> 96.4 us
    psum x4 -> x0, blocking collectives: 34.9 us -> none  [by_axis(): x = lax.psum(x, axis)]
    unnamed x0 -> x4, blocking collectives: none -> 32.2 us
    unnamed x21 -> x49, local copies, waits for them, and re-layouts: 0.85 us -> 14.5 us
    reduce_sum x0 -> x8, other arithmetic: none -> 4.87 us  [by_axis(): x = terms.sum(axis=0)]
where the time goes in v1:
time: 260 us; the launch traced here: 258 us
  blocking collectives  96.4 us (37%)
  local copies, waits for them, and re-layouts  65.1 us (25%)
  waiting for transfers between devices  51.2 us (20%)
  matrix products  23.8 us (9%)
  other arithmetic  12.2 us (5%)
  starting transfers between devices  6.11 us (2%)
  between operations  3.47 us (1%)
    all_to_all x1, blocking collectives, body(): lax.all_to_all(outgoing, EXPERT, split_axis=0, concat_axis=0, tiled=True)  64.2 us
    all_to_all x1, waiting for transfers between devices, body(): lax.all_to_all(produced, EXPERT, split_axis=0, concat_axis=0, tiled=True)  51.2 us
    unnamed x4, blocking collectives  32.2 us
    unnamed x49, local copies, waits for them, and re-layouts  14.5 us
    dot_general x1, matrix products, expert_ffn(): jnp.dot(hidden, down_proj[0], preferred_element_type=jnp.float32)  14.3 us
    gather x1, local copies, waits for them, and re-layouts, body(): picked = flat_back[slot_index].reshape(token_count, 2, width)  7.53 us
    reshape x1, local copies, waits for them, and re-layouts, body(): flat_back = returned.reshape(expert_total * capacity, width)  7.42 us
    reshape x1, local copies, waits for them, and re-layouts, expert_ffn(): flat_input = received.reshape(sources * slots, width)  7.4 us
  transfers between devices with their start and end apart: 1, of which 1 were waited for; matrix products, arithmetic and copies ran while one was open for 0% of the time, Pallas kernels for 0%

profile of v1, /device:TPU:1, one launch (start us, length us, event | category | flops | bytes accessed | tf_op | source)
XLA Modules:
  0.0 258.2 jit_solution(8719359447380530503)
XLA Ops:
  0.6 0.0 copy-start
  0.6 0.0 copy-start.1
  0.7 0.0 copy-start.4
  0.7 0.8 broadcast_multiply_fusion
  1.5 0.8 copy.14
  2.3 0.1 eq.67
  2.4 0.1 eq.63
  2.6 1.5 fusion.9
  4.1 0.1 copy.13
  4.2 0.1 mul.75
  4.4 0.1 copy.16
  4.5 0.2 fusion.24
  4.8 0.2 fusion.25
  5.0 1.4 scatter_custom_fusion
  6.4 0.3 fusion.11
  6.8 0.1 concatenate.3
  6.9 4.1 %gather_fusion = bf16[384,4096]{1,0:T(8,128)(2,1)} fusion(bf16[129,4096]{1,0:T(8,128)(2,1)S(1)} %concatenate.3, s32[1024]{0:T(1024)S(1)} %pad_clamp_fusion.1), kind=kCustom, calls=%fused_computation | custom fusion | bytes 6292992 | tf_op jit(solution)/shard_map/gather | solution.py:62
  10.9 7.1 %reshape.104 = bf16[128,3,4096]{2,1,0:T(4,128)(2,1)} reshape(bf16[384,4096]{1,0:T(8,128)(2,1)} %gather_fusion) | data formatting | bytes 6291456 | tf_op jit(solution)/shard_map/reshape | solution.py:62
  18.0 64.2 %all_to_all.10 = bf16[128,3,4096]{2,1,0:T(4,128)(2,1)} all-to-all(bf16[128,3,4096]{2,1,0:T(4,128)(2,1)} %reshape.104), channel_id=1, replica_groups=mesh['expert_0'=4,'expert_1'=4,'expert_2'=4,'expert_3'=2] {'expert_0','e..., dimensions={0} | all-to-all | bytes 6291456 | tf_op jit(solution)/shard_map/all_to_all | solution.py:63
  82.2 7.4 %reshape.105 = bf16[384,4096]{1,0:T(8,128)(2,1)} reshape(bf16[128,3,4096]{2,1,0:T(4,128)(2,1)} %all_to_all.10) | data formatting | bytes 6291456 | tf_op jit(solution)/shard_map/reshape | solution.py:19
  89.6 7.4 %fusion.4 = f32[384,768]{1,0:T(8,128)} fusion(bf16[384,4096]{1,0:T(8,128)(2,1)} %reshape.105, bf16[1,4096,768]{2,1,0:T(8,128)(2,1)} %param.14), kind=kOutput, calls=%fused_computation.7 | convolution fusion | flops 2415919104 | bytes 10616832 | tf_op jit(solution)/shard_map/dot_general | solution.py:20
  97.0 14.3 %fusion.6 = bf16[384,4096]{1,0:T(8,128)(2,1)} fusion(bf16[1,768,4096]{2,1,0:T(8,128)(2,1)} %param.16, bf16[384,4096]{1,0:T(8,128)(2,1)} %reshape.105, bf16[1,4096,768]{2,1,0:T(8,128)(2,1)} %param.15, f32[384,768]{1,0:T(8,128)} %fusion.4), kind=kOutput, calls=%fused_computation.9 | convolution fusion | flops 4835180544 | bytes 20054016 | tf_op jit(solution)/shard_map/dot_general | solution.py:23
  111.2 7.1 %reshape.106 = bf16[128,3,4096]{2,1,0:T(4,128)(2,1)} reshape(bf16[384,4096]{1,0:T(8,128)(2,1)} %fusion.6) | data formatting | bytes 6291456 | tf_op jit(solution)/shard_map/reshape | solution.py:24
  118.3 6.1 %all-to-all-start.1 = ((bf16[128,3,4096]{2,1,0:T(4,128)(2,1)}), bf16[128,3,4096]{2,1,0:T(4,128)(2,1)}, u32[]{:S(2)}, u32[]{:S(2)}) async-start(bf16[128,3,4096]{2,1,0:T(4,128)(2,1)} %reshape.106), calls=%async_computation.1 | async-start | bytes 8388608 | tf_op jit(solution)/shard_map/all_to_all | solution.py:65
  124.5 0.6 dynamic-slice
  125.1 0.0 copy-done.5
  125.1 0.5 select_reduce_fusion.1
  125.6 51.2 %all-to-all-done.1 = bf16[128,3,4096]{2,1,0:T(4,128)(2,1)} async-done(((bf16[128,3,4096]{2,1,0:T(4,128)(2,1)}), bf16[128,3,4096]{2,1,0:T(4,128)(2,1)}, u32[]{:S(2)}, u32[]{:S(2)}) %all-to-all-start.1) | async-done | bytes 3145760 | tf_op jit(solution)/shard_map/all_to_all | solution.py:65
  176.8 7.4 %reshape.107 = bf16[384,4096]{1,0:T(8,128)(2,1)} reshape(bf16[128,3,4096]{2,1,0:T(4,128)(2,1)} %all-to-all-done.1) | data formatting | bytes 6291456 | tf_op jit(solution)/shard_map/reshape | solution.py:66
  184.2 7.5 %gather_fusion.1 = bf16[256,4096]{1,0:T(8,128)(2,1)} fusion(bf16[384,4096]{1,0:T(8,128)(2,1)} %reshape.107, s32[1024]{0:T(1024)S(1)} %pad_clamp_fusion), kind=kCustom, calls=%fused_computation.1 | custom fusion | bytes 4195328 | tf_op jit(solution)/shard_map/gather | solution.py:67
  191.7 3.2 %reshape.108 = bf16[128,2,4096]{2,1,0:T(2,128)(2,1)S(1)} reshape(bf16[256,4096]{1,0:T(8,128)(2,1)} %gather_fusion.1) | data formatting | bytes 4194304 | tf_op jit(solution)/shard_map/reshape | solution.py:67
  194.9 0.0 copy-start.2
  194.9 4.7 %fusion.33 = (bf16[128,1,4096]{2,1,0:T(2,128)(2,1)S(1)}, bf16[128,1,4096]{2,1,0:T(2,128)(2,1)S(1)}) fusion(bf16[128,2,4096]{2,1,0:T(2,128)(2,1)S(1)} %reshape.108), kind=kLoop, calls=%fused_computation.61 | loop fusion | bytes 4194304 | tf_op jit(solution)/shard_map/slice | solution.py:70
  199.6 0.0 copy-start.7
  199.6 0.0 copy-start.8
  199.6 0.0 copy-start.11
  199.7 0.0 copy-start.10
  199.7 0.0 copy-start.9
  199.7 4.2 %fusion.13 = bf16[128,4096]{1,0:T(8,128)(2,1)S(1)} fusion(bf16[128,4096]{1,0:T(8,128)(2,1)S(1)} %copy-done.2, bf16[128,1,4096]{2,1,0:T(2,128)(2,1)S(1)} %get-tuple-element.16, bf16[128,1,4096]{2,1,0:T(2,128)(2,1)S(1)} %get-tuple-element.15, f32[128]{0:T(128)S(1)} %get-tuple-element.18, f32[128]{0:T(128)S(1)} %get-tuple-element.17), kind=kLoop, calls=%fused_computation.17 | loop fusion | flops 4194304 | bytes 4195328 | tf_op jit(solution)/shard_map/convert_element_type | solution.py:72
  203.9 0.0 copy-start.3
  203.9 1.6 fusion.32
  205.5 1.3 dynamic-update-slice.4
  206.8 1.4 dynamic-update-slice
  208.2 0.7 dynamic-slice.1
  208.8 6.8 %all-reduce.11 = (f32[4]{0:T(128)S(1)}, f32[4]{0:T(128)S(1)}) all-reduce(f32[4]{0:T(128)S(1)} %dynamic-update-slice, f32[4]{0:T(128)S(1)} %dynamic-update-slice.4), channel_id=1, replica_groups=mesh['expert_0'=4,'expert_1'=4,'expert_2'=4,'expert_3'=2] {'expert_0'}, use_global_device_ids=true, to_apply=%add.1 | all-reduce | flops 8 | bytes 64
  215.6 0.6 reduce_sum.136
  216.2 0.6 reduce_sum.131
  216.8 1.4 dynamic-update-slice.5
  218.2 1.4 dynamic-update-slice.1
  219.6 0.7 dynamic-slice.2
  220.3 6.9 %all-reduce.10 = (f32[4]{0:T(128)S(1)}, f32[4]{0:T(128)S(1)}) all-reduce(f32[4]{0:T(128)S(1)} %dynamic-update-slice.1, f32[4]{0:T(128)S(1)} %dynamic-update-slice.5), channel_id=1, replica_groups=mesh['expert_0'=4,'expert_1'=4,'expert_2'=4,'expert_3'=2] {'expert_1'}, use_global_device_ids=true, to_apply=%add.2 | all-reduce | flops 8 | bytes 64
  227.2 0.6 reduce_sum.137
  227.8 0.6 reduce_sum.132
  228.4 1.4 dynamic-update-slice.6
  229.7 1.4 dynamic-update-slice.2
  231.2 0.7 dynamic-slice.3
  231.9 7.2 %all-reduce.9 = (f32[4]{0:T(128)S(1)}, f32[4]{0:T(128)S(1)}) all-reduce(f32[4]{0:T(128)S(1)} %dynamic-update-slice.2, f32[4]{0:T(128)S(1)} %dynamic-update-slice.6), channel_id=1, replica_groups=mesh['expert_0'=4,'expert_1'=4,'expert_2'=4,'expert_3'=2] {'expert_2'}, use_global_device_ids=true, to_apply=%add.3 | all-reduce | flops 8 | bytes 64
  239.1 0.6 reduce_sum.138
  239.7 0.6 reduce_sum.133
  240.3 1.4 dynamic-update-slice.7
  241.6 1.4 dynamic-update-slice.3
  243.1 11.3 %all-reduce.12 = (f32[2]{0:T(128)S(1)}, f32[2]{0:T(128)S(1)}) all-reduce(f32[2]{0:T(128)S(1)} %dynamic-update-slice.3, f32[2]{0:T(128)S(1)} %dynamic-update-slice.7), channel_id=1, replica_groups=mesh['expert_0'=4,'expert_1'=4,'expert_2'=4,'expert_3'=2] {'expert_3'}, use_global_device_ids=true, to_apply=%add.4 | all-reduce | flops 4 | bytes 32
  254.4 0.7 reduce_sum.139
  255.1 0.6 reduce_sum.134
  (39 shorter events, 0.2 us)
Async XLA Ops:
  0.6 124.4 %copy-start = (bf16[4096,128]{1,0:T(8,128)(2,1)S(1)}, bf16[4096,128]{1,0:T(8,128)(2,1)}, u32[]{:S(2)}) copy-start(bf16[4096,128]{1,0:T(8,128)(2,1)} %param.12) | copy-start | bytes 3145732
  0.6 5.8 %copy-start.1 = (bf16[128,4096]{1,0:T(8,128)(2,1)S(1)}, bf16[128,4096]{1,0:T(8,128)(2,1)}, u32[]{:S(2)}) copy-start(bf16[128,4096]{1,0:T(8,128)(2,1)} %param.10) | copy-start | bytes 3145732
  0.7 5.8 %copy-start.4 = (f32[4096]{0:T(1024)S(1)}, f32[4096]{0:T(1024)}, u32[]{:S(2)}) copy-start(f32[4096]{0:T(1024)} %param.11) | copy-start | bytes 49156
  118.3 6.1 %copy-start.6 = (bf16[4096]{0:T(1024)(128)(2,1)S(1)}, bf16[4096]{0:T(1024)(128)(2,1)}, u32[]{:S(2)}) copy-start(bf16[4096]{0:T(1024)(128)(2,1)} %param.17) | copy-start | bytes 24580
  118.3 6.2 %copy-start.12 = (u32[128]{0:T(128)S(1)}, u32[128]{0:T(128)}, u32[]{:S(2)}) copy-start(u32[128]{0:T(128)} %constant.53) | copy-start | bytes 1540
  118.3 6.7 %copy-start.5 = (s32[128,2]{0,1:T(2,128)S(1)}, s32[128,2]{0,1:T(2,128)}, u32[]{:S(2)}) copy-start(s32[128,2]{0,1:T(2,128)} %param.13) | copy-start | bytes 3076
  118.3 58.5 %all-to-all-start.1 = ((bf16[128,3,4096]{2,1,0:T(4,128)(2,1)}), bf16[128,3,4096]{2,1,0:T(4,128)(2,1)}, u32[]{:S(2)}, u32[]{:S(2)}) async-start(bf16[128,3,4096]{2,1,0:T(4,128)(2,1)} %reshape.106), calls=%async_computation.1 | async-start | bytes 8388608 | tf_op jit(solution)/shard_map/all_to_all | solution.py:65
  194.9 4.7 %copy-start.2 = (bf16[128,4096]{1,0:T(8,128)(2,1)S(1)}, bf16[128,4096]{1,0:T(8,128)(2,1)}, u32[]{:S(2)}) copy-start(bf16[128,4096]{1,0:T(8,128)(2,1)} %param.10) | copy-start | bytes 3145732
  199.6 4.3 %copy-start.7 = (f32[128]{0:T(128)S(1)}, f32[128]{0:T(128)}, u32[]{:S(2)}) copy-start(f32[128]{0:T(128)} %param.19) | copy-start | bytes 1540
  199.6 4.3 %copy-start.8 = (s32[128]{0:T(128)S(1)}, s32[128]{0:T(128)}, u32[]{:S(2)}) copy-start(s32[128]{0:T(128)} %param.18) | copy-start | bytes 1540
  199.6 8.5 %copy-start.11 = (u32[128]{0:T(128)S(1)}, u32[128]{0:T(128)}, u32[]{:S(2)}) copy-start(u32[128]{0:T(128)} %constant.58) | copy-start | bytes 1540
  199.7 20.0 %copy-start.10 = (u32[128]{0:T(128)S(1)}, u32[128]{0:T(128)}, u32[]{:S(2)}) copy-start(u32[128]{0:T(128)} %constant.63) | copy-start | bytes 1540
  199.7 31.5 %copy-start.9 = (u32[128]{0:T(128)S(1)}, u32[128]{0:T(128)}, u32[]{:S(2)}) copy-start(u32[128]{0:T(128)} %constant.68) | copy-start | bytes 1540
  203.9 53.2 %copy-start.3 = (bf16[128,4096]{1,0:T(8,128)(2,1)}, bf16[128,4096]{1,0:T(8,128)(2,1)S(1)}, u32[]{:S(2)}) copy-start(bf16[128,4096]{1,0:T(8,128)(2,1)S(1)} %fusion.13) | copy-start | bytes 3145732
